TPU v7x, 32 devices: a whole 2x2x4 slice. The times are simulated.
32 devices in a mesh: dp: 8 (over z, core), seq: 4 (over y, x).
Axes of the slice: x: 2, y: 2, z: 4, core: 2. Of those that a mesh axis runs over, the one named last changes fastest.
Arguments:
- layer_in: bfloat16 [8, 512, 2560], P('dp', 'seq'), may hold values from -6 to 6
- scan_in: bfloat16 [8, 512, 2560], P('dp', 'seq'), may hold values from -6 to 6
- step_size: float32 [8, 512, 40], P('dp', 'seq'), may hold values from 0.0024 to 0.041
- b_weight: bfloat16 [2560, 64], replicated, may hold values from -0.125 to 0.125
- c_weight: bfloat16 [2560, 64], replicated, may hold values from -0.125 to 0.125
- decay_rate: float32 [40], replicated, may hold values from 0.0005 to 10
- skip_gain: float32 [40], replicated, may hold values from 0.25 to 1.75
- out_grad: bfloat16 [8, 512, 2560], P('dp', 'seq'), may hold values from -6 to 6
- doc_lengths: int32 [8, 4], P('dp'), may hold values from 1 to 256, 512 in all within a row
- block_order: int32 [8, 4], P('dp'), may hold values from 0 to 3, each once within a row
Outputs:
- scan_out: bfloat16 [8, 512, 2560], P('dp', 'seq')
- b_weight_grad: float32 [2560, 64], replicated
- c_weight_grad: float32 [2560, 64], replicated
Inputs may be any that keep to these rules, and one draw needn't show every extreme that they name: `block_order`: each row holds 0 to 3 once each. `doc_lengths`: each row sums to 512; its longest document has 256 tokens.
All inputs are finite; a program needn't handle non-finite values.
Results may differ from a plain program's by a relative error of at most 0.0055.
Values sent between devices are 32-bit elements.
A program may use at most 128 MiB of HBM per device.

v0:
```python
import math
import jax
import jax.numpy as jnp
from jax import lax
from jax.sharding import PartitionSpec as P

precise = lax.Precision.HIGHEST


def link_weights(low_block, high_block, totals):
    block_count = totals.shape[0]
    places = jnp.arange(block_count, dtype=jnp.int32)
    inside = (low_block[:, None] < places[None, :]) & (places[None, :] < high_block[:, None])
    factors = jnp.where(inside[:, :, None], totals[None, :, :], jnp.float32(1.0))
    return jnp.prod(factors, axis=1) * (low_block < high_block).astype(jnp.float32)[:, None]


def per_device(
    layer_in,
    scan_in,
    step_size,
    b_weight,
    c_weight,
    decay_rate,
    skip_gain,
    out_grad,
    doc_lengths,
    block_order,
):
    row_count = scan_in.shape[1]
    head_count = decay_rate.shape[0]
    head_width = scan_in.shape[2] // head_count
    state_count = b_weight.shape[1]
    block_count = lax.axis_size("seq")
    group_count = lax.axis_size("dp")
    my_slot = lax.axis_index("seq")
    tokens = layer_in[0]
    b_mat = jnp.dot(tokens, b_weight, preferred_element_type=jnp.float32).astype(jnp.bfloat16)
    c_mat = jnp.dot(tokens, c_weight, preferred_element_type=jnp.float32).astype(jnp.bfloat16)
    b_float = b_mat.astype(jnp.float32)
    c_float = c_mat.astype(jnp.float32)
    order_row = block_order[0]
    my_block = lax.dynamic_index_in_dim(order_row, my_slot, 0, keepdims=False)
    lengths = doc_lengths[0]
    doc_ends = jnp.cumsum(lengths, dtype=jnp.int32)
    doc_starts = doc_ends - lengths
    positions = my_block * row_count + jnp.arange(row_count, dtype=jnp.int32)
    segment = jnp.sum((doc_starts[None, :] <= positions[:, None]).astype(jnp.int32), axis=1)
    begins = jnp.any(doc_starts[None, :] == positions[:, None], axis=1)
    step_sizes = step_size[0]
    log_rates = -step_sizes * decay_rate[None, :]
    offsets = jnp.arange(row_count, dtype=jnp.int32)
    lower_tri = offsets[:, None] >= offsets[None, :]
    cumlog = jnp.dot(lower_tri.astype(jnp.float32), log_rates, precision=precise)
    linked = (segment == segment[0]) & jnp.logical_not(begins[0])
    in_last = segment == segment[row_count - 1]
    entering = jnp.where(linked[:, None], jnp.exp(cumlog), jnp.float32(0.0))
    leaving = jnp.where(
        in_last[:, None], jnp.exp(cumlog[row_count - 1][None, :] - cumlog), jnp.float32(0.0)
    )
    block_total = entering[row_count - 1]
    x_heads = scan_in[0].reshape(row_count, head_count, head_width)
    grad_heads = out_grad[0].reshape(row_count, head_count, head_width)
    driven = x_heads.astype(jnp.float32) * step_sizes[:, :, None]
    pushed = driven * leaving[:, :, None]
    seen = grad_heads.astype(jnp.float32) * entering[:, :, None]
    own_state = jnp.einsum("thp,tn->hpn", pushed, b_float, precision=precise).reshape(
        head_count, head_width * state_count
    )
    own_adjoint = jnp.einsum("thp,tn->hpn", seen, c_float, precision=precise).reshape(
        head_count, head_width * state_count
    )
    all_totals = lax.all_gather(block_total[None, :], "seq", axis=0, tiled=True)
    held_slots = jnp.arange(block_count, dtype=jnp.int32)
    onehot = (order_row[None, :] == held_slots[:, None]).astype(jnp.float32)
    seq_totals = jnp.dot(onehot, all_totals, precision=precise)
    mine_vector = jnp.full((block_count,), my_block, jnp.int32)
    from_earlier = link_weights(order_row, mine_vector, seq_totals)
    from_later = link_weights(mine_vector, order_row, seq_totals)
    incoming = jnp.einsum(
        "ch,chz->hz",
        from_earlier,
        lax.all_gather(own_state[None], "seq", axis=0, tiled=True),
        precision=precise,
    )
    returning = jnp.einsum(
        "ch,chz->hz",
        from_later,
        lax.all_gather(own_adjoint[None], "seq", axis=0, tiled=True),
        precision=precise,
    )
    incoming = incoming.reshape(head_count, head_width, state_count)
    returning = returning.reshape(head_count, head_width, state_count)
    scores = jnp.einsum("tn,sn->ts", c_mat, b_mat, preferred_element_type=jnp.float32)
    causal = lower_tri & (segment[:, None] == segment[None, :])
    set_size = math.gcd(head_count, 16)
    set_count = head_count // set_size

    def per_set(set_index, totals_pair):
        out_acc, mix_acc = totals_pair
        head_first = set_index * set_size
        set_log = lax.dynamic_slice_in_dim(cumlog, head_first, set_size, 1)
        set_steps = lax.dynamic_slice_in_dim(step_sizes, head_first, set_size, 1)
        set_driven = lax.dynamic_slice_in_dim(driven, head_first, set_size, 1)
        set_inputs = lax.dynamic_slice_in_dim(x_heads, head_first, set_size, 1)
        set_cotan = lax.dynamic_slice_in_dim(grad_heads, head_first, set_size, 1)
        log_gaps = set_log.T[:, :, None] - set_log.T[:, None, :]
        decays = jnp.exp(jnp.where(causal[None], log_gaps, jnp.float32(-1e30)))
        mixed = decays * scores[None]
        y_part = jnp.einsum("hts,shp->thp", mixed, set_driven, precision=precise)
        intersect = jnp.einsum(
            "thp,shp->hts", set_cotan, set_inputs, preferred_element_type=jnp.float32
        )
        q_part = jnp.sum(decays * intersect * set_steps.T[:, None, :], axis=0)
        out_acc = lax.dynamic_update_slice_in_dim(out_acc, y_part, head_first, 1)
        return (out_acc, mix_acc + q_part)

    start_pair = (
        jnp.zeros((row_count, head_count, head_width), jnp.float32),
        jnp.zeros((row_count, row_count), jnp.float32),
    )
    y_intra, mixing = lax.fori_loop(0, set_count, per_set, start_pair)
    y_cross = jnp.einsum("tn,hpn->thp", c_float, incoming, precision=precise) * entering[:, :, None]
    y_total = y_intra + y_cross + skip_gain[None, :, None] * x_heads.astype(jnp.float32)
    scan_out = y_total.reshape(row_count, head_count * head_width).astype(jnp.bfloat16)[None]
    grad_c = jnp.dot(mixing, b_float, precision=precise) + jnp.einsum(
        "thp,hpn->tn", seen, incoming, precision=precise
    )
    grad_b = jnp.einsum("ts,tn->sn", mixing, c_float, precision=precise) + jnp.einsum(
        "thp,hpn->tn", pushed, returning, precision=precise
    )
    local_b = jnp.einsum(
        "td,tn->dn", tokens, grad_b.astype(jnp.bfloat16), preferred_element_type=jnp.float32
    )
    local_c = jnp.einsum(
        "td,tn->dn", tokens, grad_c.astype(jnp.bfloat16), preferred_element_type=jnp.float32
    )
    summed_b, summed_c = lax.psum((local_b, local_c), ("dp", "seq"))
    scale = 1.0 / (group_count * row_count * block_count)
    return (scan_out, summed_b * scale, summed_c * scale)


def solution(mesh):
    in_specs = (
        P("dp", "seq", None),
        P("dp", "seq", None),
        P("dp", "seq", None),
        P(),
        P(),
        P(),
        P(),
        P("dp", "seq", None),
        P("dp", None),
        P("dp", None),
    )
    out_specs = (P("dp", "seq", None), P(), P())
    return jax.shard_map(
        per_device, mesh=mesh, in_specs=in_specs, out_specs=out_specs, check_vma=False
    )
```

profile of v0, /device:TPU:0, one launch (start us, length us, event | category | flops | bytes accessed | tf_op | source)
XLA Modules:
  0.0 262.6 jit_solution(5989525888902868005)
XLA Ops:
  7.3 1.3 constant_dynamic-slice_fusion
  9.2 0.8 reduce-window_clone.1
  10.0 0.7 subtract_bitcast_fusion
  10.7 0.1 convert_reduce_fusion
  10.8 0.1 compare_reduce_fusion
  10.9 1.4 copy.37
  12.3 0.2 fusion.38
  12.6 0.2 slice_reduce_fusion
  12.7 0.6 fusion.50
  13.4 0.3 convolution_convert_fusion
  13.7 1.3 broadcast_compare_fusion
  15.1 0.8 fusion.28
  16.0 1.3 broadcast_in_dim_reshape.6
  17.3 0.3 copy.38
  17.6 0.6 copy-done.7
  18.2 0.3 convolution_convert_fusion.1
  18.5 0.8 fusion.25
  19.3 1.3 broadcast_in_dim_reshape.7
  20.7 1.3 convert_multiply_fusion.1
  22.0 0.8 fusion.51
  22.8 0.2 slice_reduce_fusion.1
  23.0 0.6 iota_compare_fusion.8
  23.6 0.6 compare_convert_fusion
  24.2 1.2 bitcast_multiply_fusion.1
  25.4 1.2 bitcast_multiply_fusion
  26.6 9.7 %all-gather = f32[4,1,40]{2,1,0:T(1,128)S(1)} all-gather(f32[1,1,40]{2,1,0:T(1,128)S(1)} %bitcast.112), channel_id=1, replica_groups=mesh['dp'=8,'seq'=4] {'seq'}, dimensions={0}, use_global_device_ids=true | all-gather | bytes 800 | tf_op jit(solution)/shard_map/all_gather | solution.py:73
  36.3 0.1 fusion.46
  36.5 0.1 select_reduce_fusion
  36.7 0.1 copy.44
  36.9 0.1 copy.47
  37.0 0.1 broadcast_in_dim.120
  37.1 13.5 %while.16 = (s32[]{:T(128)}, f32[128,40,64]{0,2,1:T(8,128)S(1)}, f32[128,128]{1,0:T(8,128)S(1)}, f32[128,40,64]{0,2,1:T(8,128)}, f32[128,40]{0,1:T(8,128)S(1)}, ...) while((s32[]{:T(128)}, f32[128,40,64]{0,2,1:T(8,128)S(1)}, ...), condition=%wide.region_4.5_spmd.clone, body=%wide.region_2.4_spmd.clone.sunk | while | flops 118554632 | bytes 1202889 | solution.py:122
  37.1 0.1 fusion.81
  37.2 2.1 fusion.82
  39.4 0.3 fusion.83
  39.8 0.1 fusion.81
  39.9 2.1 fusion.82
  42.0 0.3 fusion.83
  42.5 2.2 fusion.82
  44.7 0.3 fusion.83
  45.2 2.1 fusion.82
  47.4 0.3 fusion.83
  47.8 0.1 fusion.81
  47.9 2.1 fusion.82
  50.0 0.3 fusion.83
  50.6 9.0 %all-gather.4.cloned.1.call-done = f32[4,40,4096]{2,1,0:T(8,128)} async-done(((f32[1,40,4096]{2,1,0:T(8,128)}), f32[4,40,4096]{2,1,0:T(8,128)}) %all-gather.4.cloned.1.call-update) | async-done | bytes 2621456 | tf_op jit(solution)/shard_map/all_gather | solution.py:83
  59.7 8.0 %fusion.20 = f32[40,1,4096]{2,1,0:T(1,128)S(1)} fusion(f32[4,40,1]{0,2,1:T(1,128)S(1)} %copy.44, f32[4,40,4096]{2,1,0:T(8,128)} %all-gather.4.cloned.1.call-done), kind=kOutput, calls=%fused_computation.28 | convolution fusion | flops 7864320 | bytes 3277440 | tf_op jit(solution)/shard_map/ch,chz->hz/dot_general | solution.py:80
  67.6 1.2 copy.59
  68.9 1.7 reshape.147
  70.5 31.1 %all-gather.6.cloned.1.call-done = f32[4,40,4096]{2,1,0:T(8,128)} async-done(((f32[1,40,4096]{2,1,0:T(8,128)}), f32[4,40,4096]{2,1,0:T(8,128)}) %all-gather.6.cloned.1.call-update) | async-done | bytes 2621456 | tf_op jit(solution)/shard_map/all_gather | solution.py:89
  101.6 8.2 %fusion.18 = f32[40,1,4096]{2,1,0:T(1,128)S(1)} fusion(f32[4,40,1]{0,2,1:T(1,128)S(1)} %copy.47, f32[4,40,4096]{2,1,0:T(8,128)} %all-gather.6.cloned.1.call-done), kind=kOutput, calls=%fused_computation.26 | convolution fusion | flops 7864320 | bytes 3277440 | tf_op jit(solution)/shard_map/ch,chz->hz/dot_general | solution.py:86
  109.8 0.4 copy.58
  110.2 1.6 reshape.148
  111.8 4.0 %convolution_bitcast_fusion.4 = f32[128,64]{0,1:T(8,128)S(1)} fusion(f32[128,40,64]{0,2,1:T(8,128)} %bitcast.101, f32[40,64,64]{2,1,0:T(8,128)} %reshape.148), kind=kOutput, calls=%fused_computation.47 | convolution fusion | flops 251658240 | bytes 1998848 | tf_op jit(solution)/shard_map/thp,hpn->tn/dot_general | solution.py:129
  115.8 0.2 fusion.30
  116.0 1.1 convolution_bitcast_fusion.2
  117.1 2.3 convolution_bitcast_fusion.3
  119.5 0.2 fusion.31
  119.7 1.1 convolution_bitcast_fusion.1
  120.8 2.2 fusion.24
  123.0 1.1 copy.43
  124.1 129.1 %all-reduce.3.cloned.1.call-done = (f32[2560,64]{0,1:T(8,128)}, f32[2560,64]{0,1:T(8,128)}) async-done(((f32[2560,64]{0,1:T(8,128)}, f32[2560,64]{0,1:T(8,128)}), (f32[2560,64]{0,1:T(8,128)}, f32[2560,64]{0,1:T(8,128)})) %all-reduce.3.cloned.1.call-update) | async-done | bytes 1310736 | tf_op jit(solution)/shard_map/psum | solution.py:138
  253.1 2.0 broadcast_multiply_fusion.1
  255.2 0.9 broadcast_multiply_fusion
  (45 shorter events, 0.9 us)
Async XLA Ops:
  7.2 6.2 %copy-start = (bf16[1,128,2560]{2,1,0:T(8,128)(2,1)S(1)}, bf16[1,128,2560]{2,1,0:T(8,128)(2,1)}, u32[]{:S(2)}) copy-start(bf16[1,128,2560]{2,1,0:T(8,128)(2,1)} %param.12) | copy-start | bytes 1966084
  7.2 5.1 %copy-start.5 = (f32[1,128,40]{1,2,0:T(8,128)S(1)}, f32[1,128,40]{1,2,0:T(8,128)}, u32[]{:S(2)}) copy-start(f32[1,128,40]{1,2,0:T(8,128)} %param.14) | copy-start | bytes 61444
  7.2 5.1 %copy-start.10 = (f32[40]{0:T(128)S(1)}, f32[40]{0:T(128)}, u32[]{:S(2)}) copy-start(f32[40]{0:T(128)} %param.17) | copy-start | bytes 484
  7.2 6.2 %copy-start.6 = (bf16[2560,64]{0,1:T(8,128)(2,1)S(1)}, bf16[2560,64]{0,1:T(8,128)(2,1)}, u32[]{:S(2)}) copy-start(bf16[2560,64]{0,1:T(8,128)(2,1)} %param.15) | copy-start | bytes 983044
  7.2 52.4 %all-gather.4.cloned.1.call-start = ((), (), s32[]{:S(2)}) async-start(), calls=%async_computation | async-start | bytes 3276800 | tf_op jit(solution)/shard_map/all_gather | solution.py:83
  15.9 1.4 copy-start.3
  17.2 1.0 copy-start.7
  17.3 84.4 %all-gather.6.cloned.1.call-start = ((), (), s32[]{:S(2)}) async-start(), calls=%async_computation.1 | async-start | bytes 3276800 | tf_op jit(solution)/shard_map/all_gather | solution.py:89
  20.6 3.0 %copy-start.8 = (s32[1,4]{1,0:T(1,128)S(1)}, s32[1,4]{1,0:T(1,128)}, u32[]{:S(2)}) copy-start(s32[1,4]{1,0:T(1,128)} %param.21) | copy-start | bytes 52
  20.6 232.5 %all-reduce.3.cloned.1.call-start = ((), (), s32[]{:S(2)}) async-start(), calls=%async_computation.2 | async-start | bytes 2621440 | tf_op jit(solution)/shard_map/psum | solution.py:138
  50.6 17.0 %copy-start.1 = (f32[128,40,64]{0,2,1:T(8,128)}, f32[128,40,64]{0,2,1:T(8,128)S(1)}, u32[]{:S(2)}) copy-start(f32[128,40,64]{0,2,1:T(8,128)S(1)} %get-tuple-element.173) | copy-start | bytes 3932164
  115.8 1.3 copy-start.2
  119.7 1.1 copy-start.9
  253.1 2.0 copy-start.4
Sparse Core Ops, SparseCore 0:
  17.4 42.2 all-gather.3
  62.1 39.5 all-gather.5
  120.9 132.1 all-reduce.2
where the time goes:
time: 263 us
  waiting for transfers between devices  169 us (64%)
  matrix products  43.1 us (16%)
  between operations  14.7 us (6%)
  local copies, waits for them, and re-layouts  13.5 us (5%)
  other arithmetic  11.7 us (4%)
  blocking collectives  9.7 us (4%)
    psum x1, waiting for transfers between devices, per_device(): summed_b, summed_c = lax.psum((local_b, local_c), ('dp', 'seq'))  129 us
    all_gather x1, waiting for transfers between devices, per_device(): lax.all_gather(own_adjoint[None], 'seq', axis=0, tiled=True)  31.1 us
    dot_general x5, matrix products, per_set(): y_part = jnp.einsum('hts,shp->thp', mixed, set_driven, precision=precise)  10.7 us
    all_gather x1, blocking collectives, per_device(): all_totals = lax.all_gather(block_total[None, :], 'seq', axis=0, tiled=True)  9.7 us
    all_gather x1, waiting for transfers between devices, per_device(): lax.all_gather(own_state[None], 'seq', axis=0, tiled=True)  9.04 us
    dot_general x1, matrix products, per_device(): jnp.einsum('ch,chz->hz', from_later, lax.all_gather(own_adjoint[None], 's...  8.21 us
    dot_general x1, matrix products, per_device(): jnp.einsum('ch,chz->hz', from_earlier, lax.all_gather(own_state[None], 's...  7.98 us
  transfers between devices with their start and end apart: 3, of which 3 were waited for; matrix products, arithmetic and copies ran while one was open for 14% of the time, Pallas kernels for 0%

commit v1 on v0

--- a/solution.py
+++ b/solution.py
@@ -83,12 +83,27 @@
         lax.all_gather(own_state[None], "seq", axis=0, tiled=True),
         precision=precise,
     )
-    returning = jnp.einsum(
+    size, index = (lax.axis_size("seq"), lax.axis_index("seq"))
+    behind = [(i, (i - 1) % size) for i in range(size)]
+    rows = own_adjoint[None].shape[0]
+    held = own_adjoint[None]
+    subtotal = jnp.einsum(
         "ch,chz->hz",
-        from_later,
-        lax.all_gather(own_adjoint[None], "seq", axis=0, tiled=True),
+        lax.dynamic_slice_in_dim(from_later, index * rows, held.shape[0], axis=0),
+        held,
         precision=precise,
     )
+    for lap in range(1, size):
+        held = lax.ppermute(held, "seq", behind)
+        subtotal = subtotal + jnp.einsum(
+            "ch,chz->hz",
+            lax.dynamic_slice_in_dim(
+                from_later, (index + lap) % size * rows, held.shape[0], axis=0
+            ),
+            held,
+            precision=precise,
+        )
+    returning = subtotal
     incoming = incoming.reshape(head_count, head_width, state_count)
     returning = returning.reshape(head_count, head_width, state_count)
     scores = jnp.einsum("tn,sn->ts", c_mat, b_mat, preferred_element_type=jnp.float32)

time: 263 us -> 266 us (1.011)
  starting transfers between devices: 0.12 us -> 6.82 us
  waiting for transfers between devices: 169 us -> 164 us
  local copies, waits for them, and re-layouts: 13.5 us -> 17.1 us
    ppermute x0 -> x3, waiting for transfers between devices: none -> 34.3 us  [per_device(): held = lax.ppermute(held, 'seq', behind)]
    all_gather x1 -> x0, waiting for transfers between devices: 31.1 us -> none  [per_device(): lax.all_gather(own_adjoint[None], 'seq', axis=0, tiled=True)]
    all_gather x1, waiting for transfers between devices: 9.04 us -> 0.01 us  [per_device(): lax.all_gather(own_state[None], 'seq', axis=0, tiled=True)]
    dot_general x1 -> x0, matrix products: 8.21 us -> none  [per_device(): jnp.einsum('ch,chz->hz', from_later, lax.all_gather(own_adjoint[None], 's...]
    ppermute x0 -> x3, starting transfers between devices: none -> 6.74 us  [per_device(): held = lax.ppermute(held, 'seq', behind)]
    dot_general x5, matrix products: 10.7 us -> 14.2 us  [per_set(): y_part = jnp.einsum('hts,shp->thp', mixed, set_driven, precision=precise)]
  transfers between devices with their start and end apart: 3 -> 5, of which waited for: 3 -> 3; matrix products, arithmetic and copies ran while one was open for 14% -> 16% of each run, Pallas kernels for 0% -> 0%
where the time goes in v1:
time: 266 us; the launch traced here: 265 us
  waiting for transfers between devices  164 us (62%)
  matrix products  42 us (16%)
  local copies, waits for them, and re-layouts  17.1 us (6%)
  between operations  14.9 us (6%)
  other arithmetic  12.4 us (5%)
  blocking collectives  7.22 us (3%)
  starting transfers between devices  6.82 us (3%)
    psum x1, waiting for transfers between devices, per_device(): summed_b, summed_c = lax.psum((local_b, local_c), ('dp', 'seq'))  130 us
    ppermute x3, waiting for transfers between devices, per_device(): held = lax.ppermute(held, 'seq', behind)  34.3 us
    dot_general x5, matrix products, per_set(): y_part = jnp.einsum('hts,shp->thp', mixed, set_driven, precision=precise)  14.2 us
    dot_general x1, matrix products, per_device(): jnp.einsum('ch,chz->hz', from_earlier, lax.all_gather(own_state[None], 's...  7.97 us
    all_gather x1, blocking collectives, per_device(): all_totals = lax.all_gather(block_total[None, :], 'seq', axis=0, tiled=True)  7.22 us
    ppermute x3, starting transfers between devices, per_device(): held = lax.ppermute(held, 'seq', behind)  6.74 us
  transfers between devices with their start and end apart: 5, of which 3 were waited for; matrix products, arithmetic and copies ran while one was open for 16% of the time, Pallas kernels for 0%

profile of v1, /device:TPU:0, one launch (start us, length us, event | category | flops | bytes accessed | tf_op | source)
XLA Modules:
  0.0 265.1 jit_solution(14909201139839535621)
XLA Ops:
  7.2 1.3 constant_dynamic-slice_fusion.4
  9.1 0.8 reduce-window_clone.1
  10.0 0.7 subtract_bitcast_fusion
  10.6 0.1 convert_reduce_fusion
  10.7 0.1 compare_reduce_fusion
  10.8 0.6 fusion.55
  11.4 1.0 fusion.39
  12.4 0.2 slice_reduce_fusion
  12.6 1.4 copy.38
  14.0 0.3 convolution_convert_fusion.1
  14.4 1.3 broadcast_compare_fusion
  15.8 0.8 fusion.23
  16.6 1.3 broadcast_in_dim_reshape.7
  17.8 3.9 %collective-permute-start = (f32[1,40,4096]{2,1,0:T(8,128)}, f32[1,40,4096]{2,1,0:T(8,128)}, u32[]{:S(2)}, u32[]{:S(2)}) collective-permute-start(f32[1,40,4096]{2,1,0:T(8,128)} %broadcast_in_dim_reshape.7), channel_id=1, source_target_pairs={{0,3},{1,0},{2,1},{3,2},{4,7},{5,4},{6,5},{7,6},{8,11},{9,8},{10,9... | collective-permute-start | bytes 1966088 | tf_op jit(solution)/shard_map/ppermute | solution.py:97
  21.7 1.4 copy.37
  23.2 1.3 convolution_convert_fusion
  24.5 1.9 fusion.26
  26.4 2.6 broadcast_in_dim_reshape.6
  29.0 1.3 convert_multiply_fusion.1
  30.3 0.8 fusion.56
  31.1 1.2 broadcast_in_dim.120
  32.4 16.7 %while.16 = (s32[]{:T(128)}, f32[128,40,64]{0,2,1:T(8,128)}, f32[128,128]{1,0:T(8,128)S(1)}, f32[128,40,64]{0,2,1:T(8,128)}, f32[128,40]{0,1:T(8,128)S(1)}, /*in...) while((s32[]{:T(128)}, f32[128,40,64]{0,2,1:T(8,128)}, ...), condition=%wide.region_4.5_spmd.clone, body=%wide.region_2.4_spmd.clone.sunk | while | flops 118554632 | bytes 1202881 | solution.py:137
  32.4 2.8 %fusion.86 = f32[128,40,64]{0,2,1:T(8,128)} fusion(f32[128,40,64]{0,2,1:T(8,128)} %get-tuple-element.347, s32[]{:T(128)S(6)} %select_n.91, f32[128,128]{1,0:T(8,128)} %get-tuple-element.365, f32[8,128]{1,0:T(8,128)S(1)} %get-tuple-element.330, f32[128,40,64]{0,2,1:T(8,128)} %get-tuple-element.363, pred[128,128]{1,0:T(8,128)(4,1)S(1)} %fusion.85), kind=kOutput, calls=%fused_computation.5.clone.1 | convolution fusion | flops 101056512 | bytes 615424 | tf_op jit(solution)/shard_map/while/body/eval_jaxpr/hts,shp->thp/dot_general | solution.py:125
  35.3 0.3 fusion.87
  35.8 2.8 %fusion.86 = f32[128,40,64]{0,2,1:T(8,128)} fusion(f32[128,40,64]{0,2,1:T(8,128)} %get-tuple-element.347, s32[]{:T(128)S(6)} %select_n.91, f32[128,128]{1,0:T(8,128)} %get-tuple-element.365, f32[8,128]{1,0:T(8,128)S(1)} %get-tuple-element.330, f32[128,40,64]{0,2,1:T(8,128)} %get-tuple-element.363, pred[128,128]{1,0:T(8,128)(4,1)S(1)} %fusion.85), kind=kOutput, calls=%fused_computation.5.clone.1 | convolution fusion | flops 101056512 | bytes 615424 | tf_op jit(solution)/shard_map/while/body/eval_jaxpr/hts,shp->thp/dot_general | solution.py:125
  38.6 0.3 fusion.87
  39.0 0.1 fusion.85
  39.1 2.8 %fusion.86 = f32[128,40,64]{0,2,1:T(8,128)} fusion(f32[128,40,64]{0,2,1:T(8,128)} %get-tuple-element.347, s32[]{:T(128)S(6)} %select_n.91, f32[128,128]{1,0:T(8,128)} %get-tuple-element.365, f32[8,128]{1,0:T(8,128)S(1)} %get-tuple-element.330, f32[128,40,64]{0,2,1:T(8,128)} %get-tuple-element.363, pred[128,128]{1,0:T(8,128)(4,1)S(1)} %fusion.85), kind=kOutput, calls=%fused_computation.5.clone.1 | convolution fusion | flops 101056512 | bytes 615424 | tf_op jit(solution)/shard_map/while/body/eval_jaxpr/hts,shp->thp/dot_general | solution.py:125
  42.0 0.3 fusion.87
  42.5 2.8 %fusion.86 = f32[128,40,64]{0,2,1:T(8,128)} fusion(f32[128,40,64]{0,2,1:T(8,128)} %get-tuple-element.347, s32[]{:T(128)S(6)} %select_n.91, f32[128,128]{1,0:T(8,128)} %get-tuple-element.365, f32[8,128]{1,0:T(8,128)S(1)} %get-tuple-element.330, f32[128,40,64]{0,2,1:T(8,128)} %get-tuple-element.363, pred[128,128]{1,0:T(8,128)(4,1)S(1)} %fusion.85), kind=kOutput, calls=%fused_computation.5.clone.1 | convolution fusion | flops 101056512 | bytes 615424 | tf_op jit(solution)/shard_map/while/body/eval_jaxpr/hts,shp->thp/dot_general | solution.py:125
  45.3 0.3 fusion.87
  45.7 0.1 fusion.85
  45.8 2.8 %fusion.86 = f32[128,40,64]{0,2,1:T(8,128)} fusion(f32[128,40,64]{0,2,1:T(8,128)} %get-tuple-element.347, s32[]{:T(128)S(6)} %select_n.91, f32[128,128]{1,0:T(8,128)} %get-tuple-element.365, f32[8,128]{1,0:T(8,128)S(1)} %get-tuple-element.330, f32[128,40,64]{0,2,1:T(8,128)} %get-tuple-element.363, pred[128,128]{1,0:T(8,128)(4,1)S(1)} %fusion.85), kind=kOutput, calls=%fused_computation.5.clone.1 | convolution fusion | flops 101056512 | bytes 615424 | tf_op jit(solution)/shard_map/while/body/eval_jaxpr/hts,shp->thp/dot_general | solution.py:125
  48.7 0.3 fusion.87
  49.0 1.3 reshape.174
  50.3 0.1 bitcast_multiply_fusion.1
  50.5 1.2 bitcast_multiply_fusion
  51.6 0.2 slice_reduce_fusion.1
  51.8 7.2 %all-gather = f32[4,1,40]{2,1,0:T(1,128)S(1)} all-gather(f32[1,1,40]{2,1,0:T(1,128)S(1)} %bitcast.130), channel_id=1, replica_groups=mesh['dp'=8,'seq'=4] {'seq'}, dimensions={0}, use_global_device_ids=true | all-gather | bytes 800 | tf_op jit(solution)/shard_map/all_gather | solution.py:73
  59.0 0.6 iota_compare_fusion.8
  59.6 1.5 collective-permute-start.1
  61.1 0.6 compare_convert_fusion
  61.8 0.1 fusion.47
  61.9 20.0 %collective-permute-done.1 = f32[1,40,4096]{2,1,0:T(8,128)S(1)} collective-permute-done((f32[1,40,4096]{2,1,0:T(8,128)}, f32[1,40,4096]{2,1,0:T(8,128)S(1)}, u32[]{:S(2)}, u32[]{:S(2)}) %collective-permute-start.1) | collective-permute-done | bytes 655392 | tf_op jit(solution)/shard_map/ppermute | solution.py:97
  81.9 1.3 collective-permute-start.2
  83.2 0.1 select_reduce_fusion
  83.4 0.1 copy.44
  83.6 14.3 %collective-permute-done.2 = f32[1,40,4096]{2,1,0:T(8,128)} collective-permute-done((f32[1,40,4096]{2,1,0:T(8,128)S(1)}, f32[1,40,4096]{2,1,0:T(8,128)}, u32[]{:S(2)}, u32[]{:S(2)}) %collective-permute-start.2) | collective-permute-done | bytes 655392 | tf_op jit(solution)/shard_map/ppermute | solution.py:97
  97.9 1.9 fusion.30
  99.8 1.6 reshape.181
  101.4 3.6 %convolution_bitcast_fusion.4 = f32[128,64]{0,1:T(8,128)S(1)} fusion(f32[128,40,64]{0,2,1:T(8,128)S(1)} %bitcast.121, f32[40,64,64]{2,1,0:T(8,128)} %reshape.181), kind=kOutput, calls=%fused_computation.45 | convolution fusion | flops 251658240 | bytes 1998848 | tf_op jit(solution)/shard_map/thp,hpn->tn/dot_general | solution.py:144
  105.0 0.2 fusion.28
  105.2 1.1 convolution_bitcast_fusion.2
  106.3 8.0 %fusion.18 = f32[40,1,4096]{2,1,0:T(1,128)S(1)} fusion(f32[4,40,1]{0,2,1:T(1,128)S(1)} %copy.44, f32[4,40,4096]{2,1,0:T(8,128)} %all-gather.3.cloned.1.call-done), kind=kOutput, calls=%fused_computation.26 | convolution fusion | flops 7864320 | bytes 3277440 | tf_op jit(solution)/shard_map/ch,chz->hz/dot_general | solution.py:80
  114.3 1.2 copy.52
  115.5 1.6 reshape.172
  117.1 3.6 %convolution_bitcast_fusion.3 = f32[128,64]{0,1:T(8,128)S(1)} fusion(f32[128,40,64]{0,2,1:T(8,128)} %bitcast.120, f32[40,64,64]{2,1,0:T(8,128)S(1)} %reshape.172), kind=kOutput, calls=%fused_computation.44 | convolution fusion | flops 251658240 | bytes 1998848 | tf_op jit(solution)/shard_map/thp,hpn->tn/dot_general | solution.py:141
  120.7 0.2 fusion.29
  120.9 1.1 convolution_bitcast_fusion.1
  122.1 2.2 fusion.22
  124.2 1.1 copy.43
  125.3 130.0 %all-reduce.3.cloned.1.call-done = (f32[2560,64]{0,1:T(8,128)}, f32[2560,64]{0,1:T(8,128)}) async-done(((f32[2560,64]{0,1:T(8,128)}, f32[2560,64]{0,1:T(8,128)}), (f32[2560,64]{0,1:T(8,128)}, f32[2560,64]{0,1:T(8,128)})) %all-reduce.3.cloned.1.call-update) | async-done | bytes 1310736 | tf_op jit(solution)/shard_map/psum | solution.py:153
  255.3 2.0 broadcast_multiply_fusion
  257.4 0.9 broadcast_multiply_fusion.1
  (40 shorter events, 0.8 us)
Async XLA Ops:
  7.2 6.9 %copy-start = (bf16[1,128,2560]{2,1,0:T(8,128)(2,1)S(1)}, bf16[1,128,2560]{2,1,0:T(8,128)(2,1)}, u32[]{:S(2)}) copy-start(bf16[1,128,2560]{2,1,0:T(8,128)(2,1)} %param.12) | copy-start | bytes 1966084
  7.2 6.9 %copy-start.4 = (bf16[2560,64]{0,1:T(8,128)(2,1)S(1)}, bf16[2560,64]{0,1:T(8,128)(2,1)}, u32[]{:S(2)}) copy-start(bf16[2560,64]{0,1:T(8,128)(2,1)} %param.16) | copy-start | bytes 983044
  7.2 99.1 %all-gather.3.cloned.1.call-start = ((), (), s32[]{:S(2)}) async-start(), calls=%async_computation | async-start | bytes 3276800 | tf_op jit(solution)/shard_map/all_gather | solution.py:83
  17.8 6.7 %copy-start.3 = (f32[1,128,40]{1,2,0:T(8,128)S(1)}, f32[1,128,40]{1,2,0:T(8,128)}, u32[]{:S(2)}) copy-start(f32[1,128,40]{1,2,0:T(8,128)} %param.14) | copy-start | bytes 61444
  17.8 41.8 %collective-permute-start = (f32[1,40,4096]{2,1,0:T(8,128)}, f32[1,40,4096]{2,1,0:T(8,128)}, u32[]{:S(2)}, u32[]{:S(2)}) collective-permute-start(f32[1,40,4096]{2,1,0:T(8,128)} %broadcast_in_dim_reshape.7), channel_id=1, source_target_pairs={{0,3},{1,0},{2,1},{3,2},{4,7},{5,4},{6,5},{7,6},{8,11},{9,8},{10,9... | collective-permute-start | bytes 1966088 | tf_op jit(solution)/shard_map/ppermute | solution.py:97
  29.0 226.4 %all-reduce.3.cloned.1.call-start = ((), (), s32[]{:S(2)}) async-start(), calls=%async_computation.1 | async-start | bytes 2621440 | tf_op jit(solution)/shard_map/psum | solution.py:153
  50.4 10.7 %copy-start.5 = (s32[1,4]{1,0:T(1,128)S(1)}, s32[1,4]{1,0:T(1,128)}, u32[]{:S(2)}) copy-start(s32[1,4]{1,0:T(1,128)} %param.21) | copy-start | bytes 52
  59.6 22.3 %collective-permute-start.1 = (f32[1,40,4096]{2,1,0:T(8,128)}, f32[1,40,4096]{2,1,0:T(8,128)S(1)}, u32[]{:S(2)}, u32[]{:S(2)}) collective-permute-start(f32[1,40,4096]{2,1,0:T(8,128)} %collective-permute-done), channel_id=1, source_target_pairs={{0,3},{1,0},{2,1},{3,2},{4,7},{5,4},{6,5},{7,6},{8,11},{9,8},{10,9... | collective-permute-start | bytes 1966088 | tf_op jit(solution)/shard_map/ppermute | solution.py:97
  81.9 16.0 %copy-start.2 = (f32[1,40,4096]{2,1,0:T(8,128)}, f32[1,40,4096]{2,1,0:T(8,128)S(1)}, u32[]{:S(2)}) copy-start(f32[1,40,4096]{2,1,0:T(8,128)S(1)} %collective-permute-done.1) | copy-start | bytes 1966084
  81.9 16.0 %collective-permute-start.2 = (f32[1,40,4096]{2,1,0:T(8,128)S(1)}, f32[1,40,4096]{2,1,0:T(8,128)}, u32[]{:S(2)}, u32[]{:S(2)}) collective-permute-start(f32[1,40,4096]{2,1,0:T(8,128)S(1)} %collective-permute-done.1), channel_id=1, source_target_pairs={{0,3},{1,0},{2,1},{3,2},{4,7},{5,4},{6,5},{7,6},{8,11},{9,8},{10,9... | collective-permute-start | bytes 1966088 | tf_op jit(solution)/shard_map/ppermute | solution.py:97
  120.9 1.1 copy-start.6
  255.3 2.0 copy-start.1
Sparse Core Ops, SparseCore 0:
  29.1 45.4 all-gather.2
  122.2 133.1 all-reduce.2
